TPU v7x, 8 devices: a whole 2x2x1 slice. The times are simulated.
8 devices in a mesh: dp: 8 (over z, y, x, core).
Axes of the slice: x: 2, y: 2, z: 1, core: 2. Of those that a mesh axis runs over, the one named last changes fastest.
Arguments:
- x_in: bfloat16 [32768, 896], P('dp')
- dy_mid: bfloat16 [32768, 4864], P('dp')
- x_mid: bfloat16 [32768, 4864], P('dp')
- dy_out: bfloat16 [32768, 896], P('dp')
- w_fc1: float32 [896, 4864], replicated
- w_fc2: float32 [4864, 896], replicated
- stat_left: float32 [40, 512, 512], P('dp')
- stat_right: float32 [40, 512, 512], P('dp')
- root_left: float32 [40, 512, 512], P('dp')
- root_right: float32 [40, 512, 512], P('dp')
- graft_sq: float32 [40, 512, 512], P('dp')
- momentum: float32 [40, 512, 512], P('dp')
Outputs:
- output 1: float32 [896, 4864], replicated
- output 2: float32 [4864, 896], replicated
- output 3: float32 [40, 512, 512], P('dp')
- output 4: float32 [40, 512, 512], P('dp')
- output 5: float32 [40, 512, 512], P('dp')
- output 6: float32 [40, 512, 512], P('dp')
All inputs are finite; a program needn't handle non-finite values.
Results may differ from a plain program's by a relative error of at most 0.001.
Values are sent between devices in bfloat16 or wider.
A program may use at most 1 GiB of HBM per device.

v0:
```python
import jax
import jax.numpy as jnp
from jax import lax
from jax.sharding import PartitionSpec as P

STEP = 10
STAT_DECAY = 0.999
MOM_DECAY = 0.9
GRAFT_EPS = 1e-8
LEARN_RATE = 0.01
WEIGHT_DECAY = 1e-4
BIAS_CORR = 1.0 - STAT_DECAY ** STEP


def grad_blocks(x_rows, dy_rows, block_dim):
    n_tok, n_in = x_rows.shape
    n_out = dy_rows.shape[1]
    in_blocks = -(-n_in // block_dim)
    out_blocks = -(-n_out // block_dim)
    x_pad = jnp.pad(x_rows, ((0, 0), (0, in_blocks * block_dim - n_in))).reshape(n_tok, in_blocks, block_dim)
    dy_pad = jnp.pad(dy_rows, ((0, 0), (0, out_blocks * block_dim - n_out))).reshape(n_tok, out_blocks, block_dim)
    grad_tiles = jnp.einsum('tri,tcj->rcij', x_pad, dy_pad, preferred_element_type=jnp.float32)
    return grad_tiles.reshape(in_blocks * out_blocks, block_dim, block_dim)


def from_blocks(dir_blocks, n_rows, n_cols):
    block_dim = dir_blocks.shape[-1]
    row_blocks = -(-n_rows // block_dim)
    col_blocks = -(-n_cols // block_dim)
    full_mat = dir_blocks.reshape(row_blocks, col_blocks, block_dim, block_dim).transpose(0, 2, 1, 3)
    return full_mat.reshape(row_blocks * block_dim, col_blocks * block_dim)[:n_rows, :n_cols]


def keep_mask(block_ids, n_model, n_hidden, block_dim):
    model_blocks = -(-n_model // block_dim)
    hidden_blocks = -(-n_hidden // block_dim)
    half_count = model_blocks * hidden_blocks
    is_first = block_ids < half_count
    local_ids = block_ids % half_count
    row_first = jnp.minimum(n_model - (local_ids // hidden_blocks) * block_dim, block_dim)
    col_first = jnp.minimum(n_hidden - (local_ids % hidden_blocks) * block_dim, block_dim)
    row_second = jnp.minimum(n_hidden - (local_ids // model_blocks) * block_dim, block_dim)
    col_second = jnp.minimum(n_model - (local_ids % model_blocks) * block_dim, block_dim)
    row_count = jnp.where(is_first, row_first, row_second)
    col_count = jnp.where(is_first, col_first, col_second)
    offsets = jnp.arange(block_dim)
    return (offsets[None, :, None] < row_count[:, None, None]) & (offsets[None, None, :] < col_count[:, None, None])


def stat_update(grad_blk, stat_left, stat_right):
    left_prod = jnp.einsum('nik,njk->nij', grad_blk, grad_blk, precision=lax.Precision.HIGHEST, preferred_element_type=jnp.float32)
    right_prod = jnp.einsum('nki,nkj->nij', grad_blk, grad_blk, precision=lax.Precision.HIGHEST, preferred_element_type=jnp.float32)
    return STAT_DECAY * stat_left + (1.0 - STAT_DECAY) * left_prod, STAT_DECAY * stat_right + (1.0 - STAT_DECAY) * right_prod


def direction_update(grad_blk, root_left, root_right, graft_sq, momentum, keep_tiles):
    left_mul = jnp.einsum('nij,njk->nik', root_left, grad_blk, precision=lax.Precision.HIGHEST, preferred_element_type=jnp.float32)
    precond = jnp.einsum('nij,njk->nik', left_mul, root_right, precision=lax.Precision.HIGHEST, preferred_element_type=jnp.float32)
    precond = jnp.where(keep_tiles, precond, 0.0)
    new_sq = STAT_DECAY * graft_sq + (1.0 - STAT_DECAY) * grad_blk * grad_blk
    graft_dir = grad_blk / (jnp.sqrt(new_sq / BIAS_CORR) + GRAFT_EPS)
    graft_norm = jnp.sqrt(jnp.sum(graft_dir * graft_dir, axis=(1, 2)))
    pre_norm = jnp.sqrt(jnp.sum(precond * precond, axis=(1, 2)))
    new_mom = MOM_DECAY * momentum + precond * (graft_norm / pre_norm)[:, None, None]
    return new_sq, new_mom


def apply_update(w_fc1, w_fc2, dir_blocks):
    n_model, n_hidden = w_fc1.shape
    half_count = dir_blocks.shape[0] // 2
    dir_fc1 = from_blocks(dir_blocks[:half_count], n_model, n_hidden)
    dir_fc2 = from_blocks(dir_blocks[half_count:], n_hidden, n_model)
    new_w1 = w_fc1 - LEARN_RATE * (dir_fc1.astype(jnp.float32) + WEIGHT_DECAY * w_fc1)
    new_w2 = w_fc2 - LEARN_RATE * (dir_fc2.astype(jnp.float32) + WEIGHT_DECAY * w_fc2)
    return new_w1, new_w2


def solution(mesh):
    n_dev = mesh.shape['dp']

    def per_device(x_in, dy_mid, x_mid, dy_out, w_fc1, w_fc2, stat_left, stat_right, root_left, root_right, graft_sq, momentum):
        block_dim = stat_left.shape[-1]
        n_model, n_hidden = w_fc1.shape
        own_count = stat_left.shape[0]
        local_grad = jnp.concatenate([grad_blocks(x_in, dy_mid, block_dim), grad_blocks(x_mid, dy_out, block_dim)], axis=0)
        own_grad = lax.psum_scatter(local_grad, 'dp', scatter_dimension=0, tiled=True) / n_dev
        block_ids = lax.axis_index('dp') * own_count + jnp.arange(own_count)
        keep_tiles = keep_mask(block_ids, n_model, n_hidden, block_dim)
        new_left, new_right = stat_update(own_grad, stat_left, stat_right)
        new_sq, new_mom = direction_update(own_grad, root_left, root_right, graft_sq, momentum, keep_tiles)
        all_dir = lax.all_gather(new_mom.astype(jnp.bfloat16), 'dp', axis=0, tiled=True)
        new_w1, new_w2 = apply_update(w_fc1, w_fc2, all_dir)
        return new_w1, new_w2, new_left, new_right, new_sq, new_mom

    row_spec = P('dp', None)
    rep_spec = P(None, None)
    tile_spec = P('dp', None, None)
    in_specs = (row_spec, row_spec, row_spec, row_spec, rep_spec, rep_spec, tile_spec, tile_spec, tile_spec, tile_spec, tile_spec, tile_spec)
    out_specs = (rep_spec, rep_spec, tile_spec, tile_spec, tile_spec, tile_spec)
    return jax.shard_map(per_device, mesh=mesh, in_specs=in_specs, out_specs=out_specs, check_vma=False)
```

profile of v0, /device:TPU:0, one launch (start us, length us, event | category | flops | bytes accessed | tf_op | source)
XLA Modules:
  0.0 895.5 jit_solution(3156233772139585756)
XLA Ops:
  7.2 49.0 %copy.42 = bf16[4096,4864]{0,1:T(8,128)(2,1)} copy(bf16[4096,4864]{1,0:T(8,128)(2,1)} %param.14) | data formatting | bytes 79691776 | tf_op args[2]
  67.0 27.8 %pad.17 = bf16[4096,5120]{0,1:T(8,128)(2,1)} pad(bf16[4096,4864]{0,1:T(8,128)(2,1)} %copy.42, bf16[]{:T(256)} %constant.76.clone.1), padding=0_0x0_256 | pad | bytes 81788928 | tf_op jit(solution)/shard_map/jit(_pad)/pad | solution.py:20
  102.4 52.0 %convolution_bitcast_fusion.1 = f32[10,2,512,512]{2,3,0,1:T(8,128)} fusion(bf16[4096,2,512,1]{0,2,3,1:T(8,128)(2,1)} %bitcast.55, bf16[4096,10,512,1]{0,2,1,3:T(8,128)(2,1)} %bitcast.49), kind=kOutput, calls=%fused_computation.4 | convolution fusion | flops 42949672960 | bytes 71303168 | tf_op jit(solution)/shard_map/tri,tcj->rcij/dot_general | solution.py:22
  154.4 22.0 %copy.44 = f32[10,2,512,512]{3,2,1,0:T(8,128)} copy(f32[10,2,512,512]{2,3,0,1:T(8,128)} %convolution_bitcast_fusion.1) | data formatting | bytes 41943040 | tf_op jit(solution)/shard_map/tri,tcj->rcij/transpose | solution.py:22
  176.4 48.7 %copy.62 = bf16[4096,4864]{0,1:T(8,128)(2,1)} copy(bf16[4096,4864]{1,0:T(8,128)(2,1)} %param.13) | data formatting | bytes 79691776
  225.1 27.8 %pad.14.clone = bf16[4096,5120]{0,1:T(8,128)(2,1)} pad(bf16[4096,4864]{0,1:T(8,128)(2,1)} %copy.62, bf16[]{:T(256)} %constant.76.clone.1), padding=0_0x0_256 | pad | bytes 81788928 | tf_op jit(solution)/shard_map/jit(_pad)/pad | solution.py:21
  271.3 52.5 %convolution_bitcast_fusion = f32[2,10,512,512]{2,3,0,1:T(8,128)} fusion(bf16[4096,10,512,1]{0,2,3,1:T(8,128)(2,1)} %bitcast.48, bf16[4096,2,512,1]{0,2,1,3:T(8,128)(2,1)} %bitcast.54), kind=kOutput, calls=%fused_computation.3 | convolution fusion | flops 42949672960 | bytes 71303168 | tf_op jit(solution)/shard_map/tri,tcj->rcij/dot_general | solution.py:22
  323.8 22.3 %copy.40 = f32[2,10,512,512]{3,2,1,0:T(8,128)} copy(f32[2,10,512,512]{2,3,0,1:T(8,128)} %convolution_bitcast_fusion) | data formatting | bytes 41943040 | tf_op jit(solution)/shard_map/tri,tcj->rcij/transpose | solution.py:22
  346.1 27.7 %pad_maximum_fusion = f32[40,512,512]{2,1,0:T(8,128)} fusion(f32[20,512,512]{2,1,0:T(8,128)} %bitcast.42, f32[20,512,512]{2,1,0:T(8,128)} %bitcast.43), kind=kLoop, calls=%fused_computation | loop fusion | flops 10485760 | bytes 83886080 | tf_op jit(solution)/shard_map/concatenate | solution.py:85
  374.1 238.4 %reduce-scatter.4.cloned.1.call-done = f32[5,512,512]{2,1,0:T(8,128)} async-done(((f32[40,512,512]{2,1,0:T(8,128)}), f32[5,512,512]{2,1,0:T(8,128)}) %reduce-scatter.4.cloned.1.call-update) | async-done | bytes 5242896
  612.5 15.1 %fusion.4 = f32[5,512,512]{1,2,0:T(8,128)S(1)} fusion(f32[5,512,512]{2,1,0:T(8,128)} %param.20, f32[5,512,512]{2,1,0:T(8,128)} %reduce-scatter.4.cloned.1.call-done), kind=kOutput, calls=%fused_computation.16 | convolution fusion | flops 8054374400 | bytes 15728640 | tf_op jit(solution)/shard_map/nij,njk->nik/dot_general | solution.py:57
  627.6 15.0 %multiply_reduce_fusion = (f32[5]{0:T(128)S(1)}, f32[5,512,512]{2,1,0:T(8,128)S(1)}) fusion(pred[5,512]{1,0:T(8,128)(4,1)S(1)} %iota_compare_fusion, pred[5,512]{1,0:T(8,128)(4,1)S(1)} %iota_compare_fusion.1, f32[5,512,512]{1,2,0:T(8,128)S(1)} %fusion.4, f32[5,512,512]{2,1,0:T(8,128)} %param.21), kind=kOutput, calls=%fused_computation.8 | convolution fusion | flops 8058306560 | bytes 15733780 | tf_op jit(solution)/shard_map/nij,njk->nik/dot_general | solution.py:58
  653.2 18.9 %copy.49 = f32[896,4864]{0,1:T(8,128)} copy(f32[896,4864]{1,0:T(8,128)} %param.16) | data formatting | bytes 34865152 | tf_op args[4]
  672.1 15.7 %multiply_add_fusion = f32[5,512,512]{2,1,0:T(8,128)} fusion(f32[5,512,512]{2,1,0:T(8,128)} %param.19, f32[5,512,512]{2,1,0:T(8,128)} %reduce-scatter.4.cloned.1.call-done), kind=kOutput, calls=%fused_computation.5 | convolution fusion | flops 8058306560 | bytes 15728640 | tf_op jit(solution)/shard_map/nki,nkj->nij/dot_general | solution.py:52
  687.8 15.6 %multiply_add_fusion.1 = f32[5,512,512]{2,1,0:T(8,128)} fusion(f32[5,512,512]{2,1,0:T(8,128)} %param.18, f32[5,512,512]{2,1,0:T(8,128)} %reduce-scatter.4.cloned.1.call-done), kind=kOutput, calls=%fused_computation.6 | convolution fusion | flops 8058306560 | bytes 15728640 | tf_op jit(solution)/shard_map/nik,njk->nij/dot_general | solution.py:51
  703.4 51.9 %all-gather.2.cloned.1.call-done = bf16[40,512,512]{2,1,0:T(8,128)(2,1)} async-done(((bf16[5,512,512]{2,1,0:T(8,128)(2,1)}), bf16[40,512,512]{2,1,0:T(8,128)(2,1)}) %all-gather.2.cloned.1.call-update) | async-done | bytes 20971536 | tf_op jit(solution)/shard_map/all_gather | solution.py:91
  755.3 15.7 %fusion.23 = (bf16[20,512,512]{2,1,0:T(8,128)(2,1)}, bf16[20,512,512]{2,1,0:T(8,128)(2,1)}) fusion(bf16[40,512,512]{2,1,0:T(8,128)(2,1)} %all-gather.2.cloned.1.call-done), kind=kLoop, calls=%fused_computation.45 | loop fusion | bytes 41943040 | tf_op jit(solution)/shard_map/slice | solution.py:72
  770.9 26.4 %copy.47 = bf16[2,10,512,512]{2,0,3,1:T(2,128)(2,1)} copy(bf16[2,10,512,512]{3,2,1,0:T(8,128)(2,1)} %bitcast.47) | data formatting | bytes 20971520 | tf_op jit(solution)/shard_map/reshape | solution.py:30
  797.3 11.4 %copy.64 = bf16[640,8,2,512]{3,1,2,0:T(8,128)(2,1)} copy(bf16[640,8,2,512]{3,2,1,0:T(2,128)(2,1)} %bitcast.50) | data formatting | bytes 20971520
  808.7 14.4 %multiply_subtract_fusion.1 = f32[896,4864]{0,1:T(8,128)} fusion(f32[896,4864]{0,1:T(8,128)} %copy.49, bf16[1024,5120]{0,1:T(8,128)(2,1)} %bitcast.52), kind=kLoop, calls=%fused_computation.2 | loop fusion | flops 21790720 | bytes 43581440 | tf_op jit(solution)/shard_map/sub | solution.py:73
  823.1 18.9 %copy.52 = f32[896,4864]{1,0:T(8,128)} copy(f32[896,4864]{0,1:T(8,128)} %multiply_subtract_fusion.1) | data formatting | bytes 34865152
  842.0 20.4 %copy.50 = bf16[10,512,2,512]{3,2,1,0:T(2,128)(2,1)} copy(bf16[10,512,2,512]{3,1,2,0:T(8,128)(2,1)} %bitcast.46) | data formatting | bytes 20971520 | tf_op jit(solution)/shard_map/transpose | solution.py:30
  862.4 11.3 %copy.65 = bf16[640,8,2,512]{3,1,2,0:T(8,128)(2,1)} copy(bf16[640,8,2,512]{3,2,1,0:T(2,128)(2,1)} %bitcast.51) | data formatting | bytes 20971520
  873.7 14.4 %multiply_subtract_fusion = f32[4864,896]{1,0:T(8,128)} fusion(f32[4864,896]{1,0:T(8,128)} %param.17, bf16[5120,1024]{1,0:T(8,128)(2,1)} %bitcast.53), kind=kLoop, calls=%fused_computation.1 | loop fusion | flops 21790720 | bytes 43581440 | tf_op jit(solution)/shard_map/sub | solution.py:74
  (29 shorter events, 47.6 us)
Async XLA Ops:
  7.2 605.3 %reduce-scatter.4.cloned.1.call-start = ((), (), s32[]{:S(2)}) async-start(), calls=%async_computation.2 | async-start | bytes 47185920
  373.8 381.4 %all-gather.2.cloned.1.call-start = ((), (), s32[]{:S(2)}) async-start(), calls=%async_computation.1 | async-start | bytes 23592960 | tf_op jit(solution)/shard_map/all_gather | solution.py:91
  612.5 30.1 %slice-start = ((s8[5242880]{0:T(1024)(128)(4,1)}), s8[4194304]{0:T(1024)(128)(4,1)S(1)}, s32[]{:S(2)}) async-start(s8[5242880]{0:T(1024)(128)(4,1)} %bitcast.44), calls=%async_computation.3 | async-start | bytes 8388608
  612.5 30.1 %slice-start.2 = ((s8[5242880]{0:T(1024)(128)(4,1)}), s8[4194304]{0:T(1024)(128)(4,1)S(1)}, s32[]{:S(2)}) async-start(s8[5242880]{0:T(1024)(128)(4,1)} %bitcast.56), calls=%async_computation.5 | async-start | bytes 8388608
  612.5 36.8 %slice-start.4 = ((s8[5242880]{0:T(1024)(128)(4,1)}), s8[4194304]{0:T(1024)(128)(4,1)S(1)}, s32[]{:S(2)}) async-start(s8[5242880]{0:T(1024)(128)(4,1)} %bitcast.58), calls=%async_computation.7 | async-start | bytes 8388608
  627.6 15.0 %slice-start.1 = ((s8[5242880]{0:T(1024)(128)(4,1)}), s8[1048576]{0:T(1024)(128)(4,1)S(1)}, s32[]{:S(2)}) async-start(s8[5242880]{0:T(1024)(128)(4,1)} %bitcast.44), calls=%async_computation.4 | async-start | bytes 2097152
  627.6 15.0 %slice-start.3 = ((s8[5242880]{0:T(1024)(128)(4,1)}), s8[1048576]{0:T(1024)(128)(4,1)S(1)}, s32[]{:S(2)}) async-start(s8[5242880]{0:T(1024)(128)(4,1)} %bitcast.56), calls=%async_computation.6 | async-start | bytes 2097152
  627.6 21.7 %slice-start.5 = ((s8[5242880]{0:T(1024)(128)(4,1)}), s8[1048576]{0:T(1024)(128)(4,1)S(1)}, s32[]{:S(2)}) async-start(s8[5242880]{0:T(1024)(128)(4,1)} %bitcast.58), calls=%async_computation.8 | async-start | bytes 2097152
Sparse Core Ops, SparseCore 0:
  374.0 238.5 reduce-scatter.3
  653.4 101.8 all-gather.1
where the time goes:
time: 909 us; the launch traced here: 895 us
  local copies, waits for them, and re-layouts  357 us (39%)
  waiting for transfers between devices  290 us (32%)
  matrix products  166 us (18%)
  other arithmetic  67.3 us (7%)
  between operations  14.6 us (2%)
    unnamed x3, waiting for transfers between devices  238 us
    unnamed x20, local copies, waits for them, and re-layouts  180 us
    dot_general x2, matrix products, grad_blocks(): jnp.einsum('tri,tcj->rcij', x_pad, dy_pad, preferred_element_type=jnp.flo...  104 us
    all_gather x1, waiting for transfers between devices, per_device(): lax.all_gather(new_mom.astype(jnp.bfloat16), 'dp', axis=0, tiled=True)  51.9 us
    transpose x2, local copies, waits for them, and re-layouts, grad_blocks(): jnp.einsum('tri,tcj->rcij', x_pad, dy_pad, preferred_element_type=jnp.flo...  44.3 us
    pad x2, local copies, waits for them, and re-layouts, grad_blocks(): jnp.pad(x_rows, ((0, 0), (0, in_blocks * block_dim - n_in)))  35.4 us
    pad x2, local copies, waits for them, and re-layouts, grad_blocks(): jnp.pad(dy_rows, ((0, 0), (0, out_blocks * block_dim - n_out)))  35.4 us
    concatenate x1, other arithmetic, per_device(): jnp.concatenate([grad_blocks(x_in, dy_mid, block_dim), grad_blocks(x_mid,...  27.7 us
  transfers between devices with their start and end apart: 2, of which 2 were waited for; matrix products, arithmetic and copies ran while one was open for 6% of the time, Pallas kernels for 0%

commit v1 on v0

v1 whole, which is shorter than its diff:
```python
import functools

import jax
import jax.numpy as jnp
from jax import lax
from jax.experimental import pallas as pl
from jax.experimental.pallas import tpu as pltpu
from jax.sharding import PartitionSpec as P

STEP = 10
STAT_DECAY = 0.999
MOM_DECAY = 0.9
GRAFT_EPS = 1e-8
LEARN_RATE = 0.01
WEIGHT_DECAY = 1e-4
BIAS_CORR = 1.0 - STAT_DECAY ** STEP

MESH = pl.DeviceIdType.MESH
ANY = pl.BlockSpec(memory_space=pl.ANY)
BLK = 512
HALF = 256
STRIPS = 20
ROWS_OF = (512, 384)
F32 = jnp.float32
BF16 = jnp.bfloat16
VMEM_MAX = 66 * 1000 * 1000


def flip(dev, mask):
    for bit in (1, 2, 4):
        if mask & bit:
            dev = dev + bit - 2 * bit * ((dev // bit) % 2)
    return dev


def send(src, dst, send_sem, recv_sem, dev):
    return pltpu.make_async_remote_copy(src_ref=src, dst_ref=dst, send_sem=send_sem, recv_sem=recv_sem, device_id=(dev,), device_id_type=MESH)


def wait_bytes(ref, sem):
    pltpu.make_async_copy(ref, ref, sem).wait()


def greet(devs):
    barrier = pltpu.get_barrier_semaphore()
    for dev in devs:
        pl.semaphore_signal(barrier, inc=1, device_id=(dev,), device_id_type=MESH)
    pl.semaphore_wait(barrier, len(devs))


def strip_of(pos):
    return pos % 2, pos // 4 + 5 * ((pos // 2) % 2)


def owner_of(grad, strip, part):
    in_chip = jnp.where(grad == 0, strip, 2 * (strip % 5) + part)
    chip = jnp.where(grad == 0, part, 2 + strip // 5)
    return chip, in_chip // 5, in_chip % 5


def reduce_kernel(x_in, dy_mid, x_mid, dy_out, first, second, home, narrow, wide, out_buf, total, relay,
                  narrow_sem, wide_sem, pair_send, pair_recv, unit_sem, relay_sem, first_sem, second_sem, home_sem):
    me = lax.axis_index('dp')
    core = me % 2
    my_x, my_y = (me // 2) % 2, me // 4
    my_chip = me // 2
    partner = flip(me, 1)

    narrow_copies = [pltpu.make_async_copy(src, narrow.at[k], narrow_sem.at[k]) for k, src in enumerate((x_in, dy_out))]

    def load(job, pos, own):
        grad, strip = strip_of(pos)
        half = core if own else 1 - core
        off = pl.multiple_of(jnp.where(strip == 9, 9 * BLK, strip * BLK + half * HALF), HALF)
        slot = job % 3
        for k, src in enumerate((dy_mid, x_mid)):
            @pl.when(grad == k)
            def _():
                pltpu.make_async_copy(src.at[:, pl.ds(off, HALF)], wide.at[slot], wide_sem.at[slot]).start()

    def load_job(job):
        @pl.when((job % 2 == 1) & (job < 39))
        def _():
            load(job, (job + 1) // 2, False)
        @pl.when(job % 2 == 0)
        def _():
            load(job, job // 2 - 1, True)
        @pl.when(job == 39)
        def _():
            load(job, 19, True)

    narrow_copies[0].start()
    load(0, 0, False)
    load(1, 1, False)
    narrow_copies[1].start()
    greet([partner, flip(me, 2), flip(me, 3), flip(me, 4), flip(me, 5)])

    def piece(pos, slot, part):
        grad, _ = strip_of(pos)
        cols = pl.ds(part * 512, ROWS_OF[part])
        return lax.dot_general(narrow[grad, :, cols], wide[slot], (((0,), (0,)), ((), ())), preferred_element_type=F32)

    def give(pos, job):
        slot = job % 3
        wait_bytes(wide.at[slot], wide_sem.at[slot])
        sent = (pos < 18) | (pos - 18 != core)

        @pl.when(sent)
        def _():
            @pl.when(pos >= 2)
            def _():
                wait_bytes(out_buf.at[pos % 2], pair_send.at[pos % 2])
            for part in (0, 1):
                out_buf[pos % 2, pl.ds(part * 512, ROWS_OF[part]), :] = piece(pos, slot, part)
            send(out_buf.at[pos % 2], total.at[pos], pair_send.at[pos % 2], pair_recv.at[pos], partner).start()

    def unit(pos, part):
        grad, strip = strip_of(pos)
        chip, own_core, idx = owner_of(grad, strip, part)
        half = jnp.where(strip == 9, 0, core)
        dif_x, dif_y = my_x != chip % 2, my_y != chip // 2
        dif_a = jnp.where(core == 0, dif_x, dif_y)
        dif_b = jnp.where(core == 0, dif_y, dif_x)
        rows = pl.ds(0, ROWS_OF[part])
        src = total.at[pos, pl.ds(part * 512, ROWS_OF[part]), :]
        return dict(chip=chip, own_core=own_core, idx=idx, half=half, dif_a=dif_a, dif_b=dif_b, rows=rows, src=src,
                    sem=unit_sem.at[pos * 2 + part], dest=chip * 2 + own_core, slot=5 * own_core + idx)

    def keep(pos, job):
        slot = job % 3
        wait_bytes(wide.at[slot], wide_sem.at[slot])

        @pl.when((pos < 18) | (pos - 18 == core))
        def _():
            wait_bytes(total.at[pos], pair_recv.at[pos])
            for part in (0, 1):
                here = pl.ds(part * 512, ROWS_OF[part])
                total[pos, here, :] = total[pos, here, :] + piece(pos, slot, part)
                u = unit(pos, part)
                near, far = u['dif_a'] & ~u['dif_b'], u['dif_a'] & u['dif_b']
                mine = ~u['dif_a'] & ~u['dif_b']

                @pl.when(near)
                def _():
                    send(u['src'], first.at[u['idx'], u['half'], u['rows'], :], u['sem'], first_sem.at[u['idx'], u['half']], u['dest']).start()

                @pl.when(far & (core == 0))
                def _():
                    send(u['src'], relay.at[u['slot'], u['rows'], :], u['sem'], relay_sem.at[u['slot']], flip(me, 2)).start()

                @pl.when(far & (core == 1))
                def _():
                    send(u['src'], relay.at[u['slot'], u['rows'], :], u['sem'], relay_sem.at[u['slot']], flip(me, 4)).start()

                @pl.when(mine & (u['own_core'] == core))
                def _():
                    pltpu.make_async_copy(u['src'], home.at[u['idx'], u['half'], u['rows'], :], u['sem']).start()

                @pl.when(mine & (u['own_core'] != core))
                def _():
                    send(u['src'], home.at[u['idx'], u['half'], u['rows'], :], u['sem'], home_sem.at[u['idx']], partner).start()

    narrow_copies[0].wait()
    load(2, 0, True)
    give(0, 0)
    narrow_copies[1].wait()

    def step(pos, carry):
        job = 2 * pos - 1
        load_job(job + 2)
        give(pos, job)

        @pl.when(pos < 19)
        def _():
            load_job(job + 3)
        keep(pos - 1, job + 1)
        return carry

    lax.fori_loop(1, STRIPS, step, 0)
    keep(19, 39)

    for slot in (0, 1):
        wait_bytes(out_buf.at[slot], pair_send.at[slot])

    def hop(pos, carry):
        @pl.when((pos < 18) | (pos - 18 == core))
        def _():
            for part in (0, 1):
                u = unit(pos, part)

                @pl.when(~u['dif_a'] & u['dif_b'])
                def _():
                    here = pl.ds(part * 512, ROWS_OF[part])
                    wait_bytes(relay.at[u['slot'], u['rows'], :], relay_sem.at[u['slot']])
                    total[pos, here, :] = total[pos, here, :] + relay[u['slot'], u['rows'], :]
                    send(u['src'], second.at[u['idx'], u['half'], u['rows'], :], u['sem'], second_sem.at[u['idx'], u['half']], u['dest']).start()
        return carry
    lax.fori_loop(0, STRIPS, hop, 0)

    def drain(pos, carry):
        @pl.when((pos < 18) | (pos - 18 == core))
        def _():
            for part in (0, 1):
                u = unit(pos, part)
                wait_bytes(u['src'], u['sem'])
        return carry
    lax.fori_loop(0, STRIPS, drain, 0)

    def arrive(idx, carry):
        in_chip = 5 * core + idx
        on_first = my_chip < 2
        strip = jnp.where(on_first, in_chip, 5 * (my_chip - 2) + in_chip // 2)
        tall = jnp.where(on_first, my_chip, in_chip % 2)
        for half in (0, 1):
            source = jnp.where(strip == 9, jnp.where(on_first, 0, 1), half)
            for part in (0, 1):
                rows = pl.ds(0, ROWS_OF[part])

                @pl.when((tall == part) & ((strip < 9) | (half == 0)))
                def _():
                    wait_bytes(first.at[idx, half, rows, :], first_sem.at[idx, half])
                    wait_bytes(second.at[idx, half, rows, :], second_sem.at[idx, half])

                    @pl.when(source != core)
                    def _():
                        wait_bytes(home.at[idx, half, rows, :], home_sem.at[idx])
        return carry
    lax.fori_loop(0, 5, arrive, 0)


def reduce_grads(x_in, dy_mid, x_mid, dy_out):
    tokens, n_model = x_in.shape
    piece = jax.ShapeDtypeStruct((5, 2, BLK, HALF), F32)
    dma = pltpu.SemaphoreType.DMA
    return pl.pallas_call(
        reduce_kernel,
        out_shape=(piece, piece, piece),
        in_specs=[ANY] * 4,
        out_specs=(ANY, ANY, ANY),
        scratch_shapes=[
            pltpu.VMEM((2, tokens, n_model), BF16),
            pltpu.VMEM((3, tokens, HALF), BF16),
            pltpu.VMEM((2, n_model, HALF), F32),
            pltpu.VMEM((STRIPS, n_model, HALF), F32),
            pltpu.VMEM((10, BLK, HALF), F32),
            dma((2,)), dma((3,)), dma((2,)), dma((STRIPS,)), dma((2 * STRIPS,)), dma((10,)), dma((5, 2)), dma((5, 2)), dma((5,)),
        ],
        compiler_params=pltpu.CompilerParams(collective_id=0, has_side_effects=True, vmem_limit_bytes=VMEM_MAX),
        name='reduce_grads',
    )(x_in, dy_mid, x_mid, dy_out)


def dot3(a, b, dims):
    a_hi, b_hi = a.astype(BF16), b.astype(BF16)
    a_lo, b_lo = (a - a_hi.astype(F32)).astype(BF16), (b - b_hi.astype(F32)).astype(BF16)
    dot = functools.partial(lax.dot_general, dimension_numbers=(dims, ((), ())), preferred_element_type=F32)
    return dot(a_hi, b_hi) + (dot(a_hi, b_lo) + dot(a_lo, b_hi))


NN = ((1,), (0,))
NT = ((1,), (1,))
TN = ((0,), (0,))


def block_kernel(scale, first, second, home, left, right, root_left, root_right, sq, mom,
                 new_left, new_right, new_sq, new_mom, direction, grad_buf):
    me = lax.axis_index('dp')
    core, chip = me % 2, me // 2
    in_chip = 5 * core + pl.program_id(0)
    on_first = chip < 2
    strip = jnp.where(on_first, in_chip, 5 * (chip - 2) + in_chip // 2)
    tall = jnp.where(on_first, chip, in_chip % 2)
    n_rows = jnp.where(tall == 0, 512, 384)
    n_cols = jnp.where(strip == 9, 256, 512)
    row = lax.broadcasted_iota(jnp.int32, (BLK, BLK), 0)
    col = lax.broadcasted_iota(jnp.int32, (BLK, BLK), 1)
    grad_t = jnp.concatenate([(home[0, k] + first[0, k]) + second[0, k] for k in (0, 1)], axis=1) * scale
    grad_t = jnp.where((row < n_rows) & (col < n_cols), grad_t, 0.0)

    @pl.when(on_first)
    def _():
        grad_buf[...] = grad_t

    @pl.when(~on_first)
    def _():
        grad_buf[...] = grad_t.T
    grad = grad_buf[...]
    nat_rows = jnp.where(on_first, n_rows, n_cols)
    nat_cols = jnp.where(on_first, n_cols, n_rows)
    keep = (row < nat_rows) & (col < nat_cols)
    pre = dot3(dot3(root_left[0], grad, NN), root_right[0], NN)
    pre = jnp.where(keep, pre, 0.0)
    sq_now = STAT_DECAY * sq[0] + (1.0 - STAT_DECAY) * grad * grad
    new_sq[0] = sq_now
    graft = grad / (jnp.sqrt(sq_now / BIAS_CORR) + GRAFT_EPS)
    ratio = jnp.sqrt(jnp.sum(graft * graft, keepdims=True)) / jnp.sqrt(jnp.sum(pre * pre, keepdims=True))
    mom_now = MOM_DECAY * mom[0] + pre * ratio
    new_mom[0] = mom_now

    @pl.when(on_first)
    def _():
        direction[0] = mom_now.astype(BF16)

    @pl.when(~on_first)
    def _():
        direction[0] = mom_now.T.astype(BF16)
    new_left[0] = STAT_DECAY * left[0] + (1.0 - STAT_DECAY) * dot3(grad, grad, NT)
    new_right[0] = STAT_DECAY * right[0] + (1.0 - STAT_DECAY) * dot3(grad, grad, TN)


def block_update(n_dev, pieces, left, right, root_left, root_right, sq, mom):
    half_spec = pl.BlockSpec((1, 2, BLK, HALF), lambda i: (i, 0, 0, 0))
    tile_spec = pl.BlockSpec((1, BLK, BLK), lambda i: (i, 0, 0))
    tile = jax.ShapeDtypeStruct(left.shape, F32)
    return pl.pallas_call(
        functools.partial(block_kernel, 1.0 / n_dev),
        grid=(left.shape[0],),
        out_shape=(tile, tile, tile, tile, jax.ShapeDtypeStruct(left.shape, BF16)),
        in_specs=[half_spec] * 3 + [tile_spec] * 6,
        out_specs=(tile_spec,) * 5,
        scratch_shapes=[pltpu.VMEM((BLK, BLK), F32)],
        compiler_params=pltpu.CompilerParams(vmem_limit_bytes=VMEM_MAX),
        name='block_update',
    )(*pieces, left, right, root_left, root_right, sq, mom)


def gather_kernel(own, dirs, sends, recvs):
    me = lax.axis_index('dp')
    core = me % 2
    partner, x_dev, y_dev, far_dev = flip(me, 1), flip(me, 2), flip(me, 4), flip(me, 6)
    greet([partner, x_dev, y_dev])

    def tall_of(block):
        in_chip = block % 10
        return jnp.where(block < 20, block // 10, in_chip % 2)

    def move(block, lane, dev, src=None):
        for part in (0, 1):
            rows = pl.ds(0, ROWS_OF[part])

            @pl.when(tall_of(block) == part)
            def _():
                ref = dirs.at[block] if src is None else src
                send(ref.at[rows, :], dirs.at[block, rows, :], sends.at[block, lane], recvs.at[block], dev).start()

    def landed(block, sem):
        for part in (0, 1):
            @pl.when(tall_of(block) == part)
            def _():
                wait_bytes(dirs.at[block, pl.ds(0, ROWS_OF[part]), :], sem)

    def begin(i, carry):
        block = me * 5 + i
        pltpu.make_async_copy(own.at[i], dirs.at[block], recvs.at[block]).start()
        move(block, 1, x_dev, own.at[i])
        move(block, 2, y_dev, own.at[i])
        move(block, 0, partner, own.at[i])
        return carry
    lax.fori_loop(0, 5, begin, 0)

    def near(i, carry):
        block = x_dev * 5 + i
        landed(block, recvs.at[block])
        @pl.when(core == 0)
        def _():
            move(block, 2, y_dev)
        move(block, 0, partner)
        block = y_dev * 5 + i
        landed(block, recvs.at[block])
        @pl.when(core == 1)
        def _():
            move(block, 1, x_dev)
        move(block, 0, partner)
        return carry
    lax.fori_loop(0, 5, near, 0)

    def far(i, carry):
        block = far_dev * 5 + i
        landed(block, recvs.at[block])
        move(block, 0, partner)
        return carry
    lax.fori_loop(0, 5, far, 0)

    def finish(i, carry):
        block = me * 5 + i
        wait_bytes(dirs.at[block], recvs.at[block])
        for lane in range(3):
            landed(block, sends.at[block, lane])
        landed(x_dev * 5 + i, sends.at[x_dev * 5 + i, 0])
        landed(y_dev * 5 + i, sends.at[y_dev * 5 + i, 0])
        landed(far_dev * 5 + i, sends.at[far_dev * 5 + i, 0])
        @pl.when(core == 0)
        def _():
            landed(x_dev * 5 + i, sends.at[x_dev * 5 + i, 2])
        @pl.when(core == 1)
        def _():
            landed(y_dev * 5 + i, sends.at[y_dev * 5 + i, 1])
        for mask in (1, 3, 5, 7):
            block = flip(me, mask) * 5 + i
            landed(block, recvs.at[block])
        return carry
    lax.fori_loop(0, 5, finish, 0)


def gather_dirs(own, n_blocks):
    dma = pltpu.SemaphoreType.DMA
    return pl.pallas_call(
        gather_kernel,
        out_shape=jax.ShapeDtypeStruct((n_blocks, BLK, BLK), BF16),
        in_specs=[ANY],
        out_specs=ANY,
        scratch_shapes=[dma((n_blocks, 3)), dma((n_blocks,))],
        compiler_params=pltpu.CompilerParams(collective_id=1, has_side_effects=True),
        name='gather_dirs',
    )(own)


def apply_kernel(flipped, dirs, w, out):
    step = dirs[0, 0].astype(F32)
    step = step.T if flipped else step
    out[...] = w[...] - LEARN_RATE * (step + WEIGHT_DECAY * w[...])


def apply_update(w, dirs, flipped):
    rows, cols = w.shape
    grid = (-(-rows // BLK), -(-cols // BLK))
    if flipped:
        index = lambda i, j: (2 + i // 5, 2 * (i % 5) + j, 0, 0)
    else:
        index = lambda i, j: (i, j, 0, 0)
    return pl.pallas_call(
        functools.partial(apply_kernel, flipped),
        grid=grid,
        out_shape=jax.ShapeDtypeStruct(w.shape, F32),
        in_specs=[pl.BlockSpec((1, 1, BLK, BLK), index), pl.BlockSpec((BLK, BLK), lambda i, j: (i, j))],
        out_specs=pl.BlockSpec((BLK, BLK), lambda i, j: (i, j)),
        compiler_params=pltpu.CompilerParams(vmem_limit_bytes=VMEM_MAX),
        name='apply_update',
    )(dirs, w)


def solution(mesh):
    n_dev = mesh.shape['dp']

    def per_device(x_in, dy_mid, x_mid, dy_out, w_fc1, w_fc2, stat_left, stat_right, root_left, root_right, graft_sq, momentum):
        pieces = reduce_grads(x_in, dy_mid, x_mid, dy_out)
        new_left, new_right, new_sq, new_mom, own = block_update(n_dev, pieces, stat_left, stat_right, root_left, root_right, graft_sq, momentum)
        dirs = gather_dirs(own, n_dev * own.shape[0]).reshape(4, 10, BLK, BLK)
        new_w1 = apply_update(w_fc1, dirs, False)
        new_w2 = apply_update(w_fc2, dirs, True)
        return new_w1, new_w2, new_left, new_right, new_sq, new_mom

    row_spec = P('dp', None)
    rep_spec = P(None, None)
    tile_spec = P('dp', None, None)
    in_specs = (row_spec, row_spec, row_spec, row_spec, rep_spec, rep_spec, tile_spec, tile_spec, tile_spec, tile_spec, tile_spec, tile_spec)
    out_specs = (rep_spec, rep_spec, tile_spec, tile_spec, tile_spec, tile_spec)
    return jax.shard_map(per_device, mesh=mesh, in_specs=in_specs, out_specs=out_specs, check_vma=False)
```

time: 909 us -> 352 us (0.39); the launches traced: 895 us -> 348 us
  local copies, waits for them, and re-layouts: 357 us -> 0 us
  Pallas kernels: 0 us -> 348 us
  waiting for transfers between devices: 290 us -> 0 us
  matrix products: 166 us -> 0 us
  other arithmetic: 67.3 us -> 0 us
  between operations: 14.6 us -> 0.65 us
    pallas_call x0 -> x5, Pallas kernels: none -> 348 us  [the longest x1 187 us: reduce_grads(): pl.pallas_call(reduce_kernel, out_shape=(piece, piece, piece), in_specs=[...]
    unnamed x3 -> x0, waiting for transfers between devices: 238 us -> none
    unnamed x20 -> x0, local copies, waits for them, and re-layouts: 180 us -> none
    dot_general x6 -> x0, matrix products: 166 us -> none  [the longest x2 104 us: grad_blocks(): jnp.einsum('tri,tcj->rcij', x_pad, dy_pad, preferred_element_type=jnp.flo...]
    pad x4 -> x0, local copies, waits for them, and re-layouts: 70.8 us -> none  [the longest x2 35.4 us: grad_blocks(): jnp.pad(x_rows, ((0, 0), (0, in_blocks * block_dim - n_in)))]
    transpose x3 -> x0, local copies, waits for them, and re-layouts: 64.7 us -> none  [the longest x2 44.3 us: grad_blocks(): jnp.einsum('tri,tcj->rcij', x_pad, dy_pad, preferred_element_type=jnp.flo...]
    all_gather x1 -> x0, waiting for transfers between devices: 51.9 us -> none  [per_device(): lax.all_gather(new_mom.astype(jnp.bfloat16), 'dp', axis=0, tiled=True)]
    sub x2 -> x0, other arithmetic: 28.9 us -> none  [the longest x1 14.4 us: apply_update(): w_fc1 - LEARN_RATE * (dir_fc1.astype(jnp.float32) + WEIGHT_DECAY * w_fc1)]
  transfers between devices with their start and end apart: 2 -> 0, of which waited for: 2 -> 0; matrix products, arithmetic and copies ran while one was open for 6% -> 0% of each run, Pallas kernels for 0% -> 0%
where the time goes in v1:
time: 352 us; the launch traced here: 348 us
  Pallas kernels  348 us (99%)
    pallas_call x1, Pallas kernels, reduce_grads(): pl.pallas_call(reduce_kernel, out_shape=(piece, piece, piece), in_specs=[...  187 us
    pallas_call x1, Pallas kernels, gather_dirs(): pl.pallas_call(gather_kernel, out_shape=jax.ShapeDtypeStruct((n_blocks, B...  82.4 us
    pallas_call x2, Pallas kernels, apply_update(): pl.pallas_call(functools.partial(apply_kernel, flipped), grid=grid, out_s...  46.3 us
    pallas_call x1, Pallas kernels, block_update(): pl.pallas_call(functools.partial(block_kernel, 1.0 / n_dev), grid=(left.s...  31.7 us

profile of v1, /device:TPU:0, one launch (start us, length us, event | category | flops | bytes accessed | tf_op | source)
XLA Modules:
  0.0 348.2 jit_solution(16467340538620601217)
XLA Ops:
  0.6 187.2 %reduce_grads.1 = (f32[5,2,512,256]{3,2,1,0:T(8,128)}, f32[5,2,512,256]{3,2,1,0:T(8,128)}, f32[5,2,512,256]{3,2,1,0:T(8,128)}) custom-call(bf16[4096,896]{1,0:T(8,128)(2,1)} %x_in.1, bf16[4096,4864]{1,0:T(8,128)(2,1)} %dy_mid.1, bf16[4096,4864]{1,0:T(8,128)(2,1)} %x_mid.1, bf16[4096,896]{1,0:T(8,128)(2,1)} %dy_out.1), custom_call_target="tpu_custom_call" | custom-call | tf_op jit(solution)/shard_map/reduce_grads/pallas_call | solution.py:235
  187.8 31.7 %block_update.1 = (f32[5,512,512]{2,1,0:T(8,128)}, f32[5,512,512]{2,1,0:T(8,128)}, f32[5,512,512]{2,1,0:T(8,128)}, f32[5,512,512]{2,1,0:T(8,128)}, bf16[5,512,512]{2,1,0:T(8,128)(2,1)}) custom-call(f32[5,2,512,256]{3,2,1,0:T(8,128)} %get-tuple-element.14.first, f32[5,2,512,256]{3,2,1,0:T(8,128)} %get-tuple-element.15.second, ...), custom_call_target="tpu_custom_call" | custom-call | tf_op jit(solution)/shard_map/block_update/pallas_call | solution.py:315
  219.5 82.4 %gather_dirs.1 = bf16[40,512,512]{2,1,0:T(8,128)(2,1)} custom-call(bf16[5,512,512]{2,1,0:T(8,128)(2,1)} %get-tuple-element.17.own), custom_call_target="tpu_custom_call" | custom-call | tf_op jit(solution)/shard_map/gather_dirs/pallas_call | solution.py:407
  301.9 23.7 %apply_update.3 = f32[4864,896]{1,0:T(8,128)} custom-call(bf16[4,10,512,512]{3,2,1,0:T(8,128)(2,1)} %bitcast.1, f32[4864,896]{1,0:T(8,128)} %w.3), custom_call_target="tpu_custom_call" | custom-call | tf_op jit(solution)/shard_map/apply_update/pallas_call | solution.py:431
  325.6 22.6 %apply_update.2 = f32[896,4864]{1,0:T(8,128)} custom-call(bf16[4,10,512,512]{3,2,1,0:T(8,128)(2,1)} %bitcast.2, f32[896,4864]{1,0:T(8,128)} %w.2), custom_call_target="tpu_custom_call" | custom-call | tf_op jit(solution)/shard_map/apply_update/pallas_call | solution.py:431

commit v2 on v0

v2 whole, which is shorter than its diff:
```python
import functools

import jax
import jax.numpy as jnp
from jax import lax
from jax.experimental import pallas as pl
from jax.experimental.pallas import tpu as pltpu
from jax.sharding import PartitionSpec as P

STEP = 10
STAT_DECAY = 0.999
MOM_DECAY = 0.9
GRAFT_EPS = 1e-8
LEARN_RATE = 0.01
WEIGHT_DECAY = 1e-4
BIAS_CORR = 1.0 - STAT_DECAY ** STEP

MESH = pl.DeviceIdType.MESH
ANY = pl.BlockSpec(memory_space=pl.ANY)
BLK = 512
HALF = 256
STRIPS = 20
LAG = 4
HOPS, HOP_FROM, SEND_FROM = 3, 2, 0
EARLY = 3
ROWS_OF = (512, 384)
F32 = jnp.float32
BF16 = jnp.bfloat16
VMEM_MAX = 66 * 1000 * 1000


def flip(dev, mask):
    for bit in (1, 2, 4):
        if mask & bit:
            dev = dev + bit - 2 * bit * ((dev // bit) % 2)
    return dev


def send(src, dst, send_sem, recv_sem, dev):
    return pltpu.make_async_remote_copy(src_ref=src, dst_ref=dst, send_sem=send_sem, recv_sem=recv_sem, device_id=(dev,), device_id_type=MESH)


def wait_bytes(ref, sem):
    pltpu.make_async_copy(ref, ref, sem).wait()


def greet(devs):
    barrier = pltpu.get_barrier_semaphore()
    for dev in devs:
        pl.semaphore_signal(barrier, inc=1, device_id=(dev,), device_id_type=MESH)
    pl.semaphore_wait(barrier, len(devs))


def strip_of(pos):
    turn, grad = pos // 4, pos % 2
    return grad, jnp.where(grad == 0, turn, (3 * turn) % 5) + 5 * ((pos // 2) % 2)


def owner_of(grad, strip, part):
    in_chip = jnp.where(grad == 0, strip, 2 * (strip % 5) + part)
    return jnp.where(grad == 0, part, 2 + strip // 5), in_chip


def slot_at(chip, core, turn):
    return jnp.where((chip >= 2) & (core == 1), (turn + 1) % 5, turn)


def tile_at(chip, in_chip):
    strip = jnp.where(chip < 2, in_chip, 5 * (chip - 2) + in_chip // 2)
    return strip, jnp.where(chip < 2, chip, in_chip % 2)


def step_kernel(scale, x_in, dy_mid, x_mid, dy_out, root_left, root_right, graft_sq, momentum, stat_left, stat_right,
                first, second, home, new_left, new_right, new_sq, new_mom, own, pair, from_a, from_c, from_b, pair_a, pair_b,
                narrow, wide, out_buf, total, relay, piece_buf, state_buf, tile_a, tile_b,
                narrow_sem, wide_sem, pair_send, pair_recv, unit_sem, relay_sem, first_sem, second_sem, home_sem,
                piece_sem, state_sem, out_sem, dir_send, dir_recv, pass_send, pass_recv):
    me = lax.axis_index('dp')
    core = me % 2
    my_x, my_y = (me // 2) % 2, me // 4
    my_chip = me // 2
    partner, x_dev, y_dev = flip(me, 1), flip(me, 2), flip(me, 4)

    narrow_copies = [pltpu.make_async_copy(src, narrow.at[k], narrow_sem.at[k]) for k, src in enumerate((x_in, dy_out))]

    def load(job, pos, own_half):
        grad, strip = strip_of(pos)
        half = core if own_half else 1 - core
        off = pl.multiple_of(jnp.where(strip == 9, 9 * BLK, strip * BLK + half * HALF), HALF)
        slot = job % 3
        for k, src in enumerate((dy_mid, x_mid)):
            @pl.when(grad == k)
            def _():
                pltpu.make_async_copy(src.at[:, pl.ds(off, HALF)], wide.at[slot], wide_sem.at[slot]).start()

    def load_job(job):
        @pl.when((job % 2 == 1) & (job < 39))
        def _():
            load(job, (job + 1) // 2, False)
        @pl.when(job % 2 == 0)
        def _():
            load(job, job // 2 - 1, True)
        @pl.when(job == 39)
        def _():
            load(job, 19, True)

    narrow_copies[0].start()
    load(0, 0, False)
    load(1, 1, False)
    narrow_copies[1].start()
    greet([partner, x_dev, flip(me, 3), y_dev, flip(me, 5)])

    def product(pos, slot):
        grad, _ = strip_of(pos)
        return lax.dot_general(narrow[grad], wide[slot], (((0,), (0,)), ((), ())), preferred_element_type=F32)

    def given(pos):
        grad, strip = strip_of(pos)
        return (strip != 9) | (grad != core)

    def kept(pos):
        grad, strip = strip_of(pos)
        return (strip != 9) | (grad == core)

    def give(pos, job):
        slot = job % 3
        wait_bytes(wide.at[slot], wide_sem.at[slot])

        @pl.when(given(pos))
        def _():
            @pl.when(pos >= 2)
            def _():
                wait_bytes(out_buf.at[pos % 2], pair_send.at[pos % 2])
            out_buf[pos % 2] = product(pos, slot)
            send(out_buf.at[pos % 2], total.at[pos], pair_send.at[pos % 2], pair_recv.at[pos], partner).start()

    def unit(pos, part):
        grad, strip = strip_of(pos)
        chip, in_chip = owner_of(grad, strip, part)
        own_core = in_chip // 5
        odd_one = in_chip % 5 == 2
        x_first = jnp.where(odd_one, chip % 2 == 1, core == 0)
        dif_x, dif_y = my_x != chip % 2, my_y != chip // 2
        slot = jnp.where(odd_one & (chip % 2 == 0), 10 + in_chip // 5, in_chip)
        return dict(idx=in_chip % 5, own_core=own_core, half=jnp.where(strip == 9, 0, core), x_first=x_first,
                    near=(dif_x & ~dif_y & x_first) | (dif_y & ~dif_x & ~x_first),
                    second=(dif_y & ~dif_x & x_first) | (dif_x & ~dif_y & ~x_first),
                    far=dif_x & dif_y, mine=~dif_x & ~dif_y,
                    rows=pl.ds(0, ROWS_OF[part]), src=total.at[pos, pl.ds(part * 512, ROWS_OF[part]), :],
                    sem=unit_sem.at[pos * 2 + part], dest=chip * 2 + own_core, slot=slot)

    def keep(pos, job):
        slot = job % 3
        wait_bytes(wide.at[slot], wide_sem.at[slot])

        @pl.when(kept(pos))
        def _():
            wait_bytes(total.at[pos], pair_recv.at[pos])
            total[pos] = total[pos] + product(pos, slot)
            for part in (0, 1):
                u = unit(pos, part)

                @pl.when(u['near'])
                def _():
                    send(u['src'], first.at[u['idx'], u['half'], u['rows'], :], u['sem'], first_sem.at[u['idx'], u['half']], u['dest']).start()

                @pl.when(u['far'] & u['x_first'])
                def _():
                    send(u['src'], relay.at[u['slot'], u['rows'], :], u['sem'], relay_sem.at[u['slot']], x_dev).start()

                @pl.when(u['far'] & ~u['x_first'])
                def _():
                    send(u['src'], relay.at[u['slot'], u['rows'], :], u['sem'], relay_sem.at[u['slot']], y_dev).start()

                @pl.when(u['mine'] & (u['own_core'] == core))
                def _():
                    pltpu.make_async_copy(u['src'], home.at[u['idx'], u['half'], u['rows'], :], u['sem']).start()

                @pl.when(u['mine'] & (u['own_core'] != core))
                def _():
                    send(u['src'], home.at[u['idx'], u['half'], u['rows'], :], u['sem'], home_sem.at[u['idx']], partner).start()

    narrow_copies[0].wait()
    load(2, 0, True)
    give(0, 0)
    narrow_copies[1].wait()

    def hop(pos, carry):
        @pl.when(kept(pos))
        def _():
            for part in (0, 1):
                u = unit(pos, part)

                @pl.when(u['second'])
                def _():
                    here = pl.ds(part * 512, ROWS_OF[part])
                    wait_bytes(relay.at[u['slot'], u['rows'], :], relay_sem.at[u['slot']])
                    total[pos, here, :] = total[pos, here, :] + relay[u['slot'], u['rows'], :]
                    send(u['src'], second.at[u['idx'], u['half'], u['rows'], :], u['sem'], second_sem.at[u['idx'], u['half']], u['dest']).start()
        return carry

    def step(pos, carry):
        job = 2 * pos - 1
        load_job(job + 2)
        give(pos, job)

        @pl.when(pos < 19)
        def _():
            load_job(job + 3)
        keep(pos - 1, job + 1)

        @pl.when(pos > LAG)
        def _():
            hop(pos - 1 - LAG, 0)
        return carry
    lax.fori_loop(1, STRIPS, step, 0)
    keep(19, 39)

    def fetch_state(turn):
        idx = slot_at(my_chip, core, turn)
        for k, src in enumerate((root_left, root_right, graft_sq, momentum, stat_left, stat_right)):
            pltpu.make_async_copy(src.at[idx], state_buf.at[k], state_sem.at[k]).start()
    fetch_state(0)

    for slot in (0, 1):
        wait_bytes(out_buf.at[slot], pair_send.at[slot])

    row = lax.broadcasted_iota(jnp.int32, (BLK, BLK), 0)
    col = lax.broadcasted_iota(jnp.int32, (BLK, BLK), 1)
    on_first = my_chip < 2
    chunk = 256

    def split(value, at):
        high = value.astype(BF16)
        narrow[1, pl.ds(at * BLK, BLK), pl.ds(0, BLK)] = high
        narrow[1, pl.ds((at + 1) * BLK, BLK), pl.ds(0, BLK)] = (value - high.astype(F32)).astype(BF16)

    def times(value, at):
        high = value.astype(BF16)
        low = (value - high.astype(F32)).astype(BF16)
        dot = functools.partial(jnp.dot, preferred_element_type=F32)
        b_high = narrow[1, pl.ds(at * BLK, BLK), pl.ds(0, BLK)]
        b_low = narrow[1, pl.ds((at + 1) * BLK, BLK), pl.ds(0, BLK)]
        return dot(high, b_high) + (dot(high, b_low) + dot(low, b_high))

    def leave(turn):
        tall = tile_at(my_chip, 5 * core + slot_at(my_chip, core, turn))[1]
        for part in (0, 1):
            rows = pl.ds(0, ROWS_OF[part])

            @pl.when(tall == part)
            def _():
                src = narrow.at[0, pl.ds(pl.multiple_of(turn * BLK, BLK), ROWS_OF[part]), pl.ds(0, BLK)]
                pltpu.make_async_copy(src, own.at[turn, rows, :], dir_send.at[0, turn]).start()
                for k, (dev_a, dev_b) in enumerate(((x_dev, y_dev), (y_dev, x_dev))):
                    @pl.when((core == k) & (turn < EARLY))
                    def _():
                        send(src, from_a.at[turn, rows, :], dir_send.at[2, turn], dir_recv.at[1, turn], dev_a).start()

                    @pl.when((core == k) & (turn >= EARLY))
                    def _():
                        send(src, from_c.at[turn - EARLY, rows, :], dir_send.at[2, turn], dir_recv.at[1, turn], dev_a).start()

                    @pl.when(core == k)
                    def _():
                        send(src, from_b.at[turn, rows, :], dir_send.at[3, turn], dir_recv.at[2, turn], dev_b).start()
                send(src, pair.at[turn, rows, :], dir_send.at[1, turn], dir_recv.at[0, turn], partner).start()

    def block(turn, carry):
        for k in range(HOPS):
            pos = STRIPS - 1 - LAG + HOPS * (turn - HOP_FROM) + k

            @pl.when((turn >= HOP_FROM) & (pos < STRIPS))
            def _():
                hop(pos, 0)
        idx = slot_at(my_chip, core, turn)
        in_chip = 5 * core + idx
        strip, tall = tile_at(my_chip, in_chip)
        for half in (0, 1):
            source = jnp.where(strip == 9, jnp.where(on_first, 0, 1), half)
            for part in (0, 1):
                rows = pl.ds(0, ROWS_OF[part])

                @pl.when((tall == part) & ((strip < 9) | (half == 0)))
                def _():
                    wait_bytes(first.at[idx, half, rows, :], first_sem.at[idx, half])
                    wait_bytes(second.at[idx, half, rows, :], second_sem.at[idx, half])

                    @pl.when(source != core)
                    def _():
                        wait_bytes(home.at[idx, half, rows, :], home_sem.at[idx])

                    @pl.when(source == core)
                    def _():
                        for grad in (0, 1):
                            @pl.when(on_first == (grad == 0))
                            def _():
                                turn5 = strip % 5 if grad == 0 else (2 * (strip % 5)) % 5
                                pos = 4 * turn5 + 2 * (strip // 5) + grad
                                wait_bytes(home.at[idx, half, rows, :], unit_sem.at[pos * 2 + part])
        for k, src in enumerate((home, first, second)):
            pltpu.make_async_copy(src.at[idx], piece_buf.at[k], piece_sem.at[k]).start()
        for k, src in enumerate((home, first, second)):
            wait_bytes(piece_buf.at[k], piece_sem.at[k])
        n_rows = jnp.where(tall == 0, 512, 384)
        n_cols = jnp.where(strip == 9, 256, 512)
        for half in (0, 1):
            here = pl.ds(half * HALF, HALF)
            value = ((piece_buf[0, half] + piece_buf[1, half]) + piece_buf[2, half]) * scale
            tile_a[:, here] = jnp.where((row[:, :HALF] < n_rows) & (col[:, :HALF] + half * HALF < n_cols), value, 0.0)

        @pl.when(on_first)
        def _():
            tile_b[...] = tile_a[...]

        @pl.when(~on_first)
        def _():
            tile_b[...] = tile_a[...].T
        for k in range(6):
            wait_bytes(state_buf.at[k], state_sem.at[k])
        split(tile_b[...], 0)
        split(state_buf[1], 2)
        nat_rows = jnp.where(on_first, n_rows, n_cols)
        nat_cols = jnp.where(on_first, n_cols, n_rows)

        def rows_step(r, sums):
            here = pl.ds(pl.multiple_of(r * chunk, chunk), chunk)
            pre = times(times(state_buf[0, here, :], 0), 2)
            pre = jnp.where((row[:chunk] + r * chunk < nat_rows) & (col[:chunk] < nat_cols), pre, 0.0)
            tile_a[here, :] = pre
            grad = tile_b[here, :]
            sq_now = STAT_DECAY * state_buf[2, here, :] + (1.0 - STAT_DECAY) * grad * grad
            state_buf[2, here, :] = sq_now
            graft = grad / (jnp.sqrt(sq_now / BIAS_CORR) + GRAFT_EPS)
            return sums[0] + jnp.sum(graft * graft, keepdims=True), sums[1] + jnp.sum(pre * pre, keepdims=True)
        zero = jnp.zeros((1, 1), F32)
        graft_sum, pre_sum = lax.fori_loop(0, BLK // chunk, rows_step, (zero, zero))
        ratio = jnp.sqrt(graft_sum) / jnp.sqrt(pre_sum)
        state_buf[3] = MOM_DECAY * state_buf[3] + tile_a[...] * ratio
        dirs = narrow.at[0, pl.ds(pl.multiple_of(turn * BLK, BLK), BLK), pl.ds(0, BLK)]

        @pl.when(on_first)
        def _():
            dirs[...] = state_buf[3].astype(BF16)

        @pl.when(~on_first)
        def _():
            dirs[...] = state_buf[3].T.astype(BF16)

        @pl.when(turn == SEND_FROM)
        def _():
            for k in range(SEND_FROM):
                leave(k)

        @pl.when(turn >= SEND_FROM)
        def _():
            leave(turn)

        def stats_step(r, carry):
            here = pl.ds(pl.multiple_of(r * chunk, chunk), chunk)
            high = narrow[1, pl.ds(0, BLK), pl.ds(0, BLK)]
            low = narrow[1, pl.ds(BLK, BLK), pl.ds(0, BLK)]
            dot = functools.partial(lax.dot_general, preferred_element_type=F32)
            nt, tn = (((1,), (1,)), ((), ())), (((0,), (0,)), ((), ()))
            a_high = narrow[1, here, pl.ds(0, BLK)]
            a_low = narrow[1, pl.ds(pl.multiple_of(BLK + r * chunk, chunk), chunk), pl.ds(0, BLK)]
            state_buf[4, here, :] = STAT_DECAY * state_buf[4, here, :] + (1.0 - STAT_DECAY) * (
                dot(a_high, high, nt) + (dot(a_high, low, nt) + dot(a_low, high, nt)))
            b_high = narrow[1, pl.ds(0, BLK), here]
            b_low = narrow[1, pl.ds(BLK, BLK), here]
            state_buf[5, here, :] = STAT_DECAY * state_buf[5, here, :] + (1.0 - STAT_DECAY) * (
                dot(b_high, high, tn) + (dot(b_high, low, tn) + dot(b_low, high, tn)))
            return carry
        lax.fori_loop(0, BLK // chunk, stats_step, 0)
        for k, dst in enumerate((new_sq, new_mom, new_left, new_right)):
            pltpu.make_async_copy(state_buf.at[2 + k], dst.at[idx], out_sem.at[k]).start()
        for k in range(4):
            wait_bytes(state_buf.at[2 + k], out_sem.at[k])

        @pl.when(turn < 4)
        def _():
            fetch_state(turn + 1)
        return carry
    lax.fori_loop(0, 5, block, 0)

    def drain(pos, carry):
        @pl.when(kept(pos))
        def _():
            for part in (0, 1):
                u = unit(pos, part)

                @pl.when(~(u['mine'] & (u['own_core'] == core)))
                def _():
                    wait_bytes(u['src'], u['sem'])
        return carry
    lax.fori_loop(0, STRIPS, drain, 0)

    x_chip, y_chip = x_dev // 2, y_dev // 2
    a_chip, b_chip = jnp.where(core == 0, x_chip, y_chip), jnp.where(core == 0, y_chip, x_chip)

    def tall_of(chip, its_core, turn):
        return tile_at(chip, 5 * its_core + slot_at(chip, its_core, turn))[1]

    def hand_on(turn, carry):
        for part in (0, 1):
            rows = pl.ds(0, ROWS_OF[part])
            ref = own.at[turn, rows, :]

            @pl.when(tall_of(a_chip, core, turn) == part)
            def _():
                wait_bytes(ref, dir_recv.at[1, turn])

                @pl.when(turn < EARLY)
                def _():
                    send(from_a.at[turn, rows, :], pair_a.at[turn, rows, :], pass_send.at[0, turn], pass_recv.at[0, turn], partner).start()

                @pl.when(turn >= EARLY)
                def _():
                    send(from_c.at[turn - EARLY, rows, :], pair_a.at[turn, rows, :], pass_send.at[0, turn], pass_recv.at[0, turn], partner).start()

            @pl.when(tall_of(b_chip, core, turn) == part)
            def _():
                wait_bytes(ref, dir_recv.at[2, turn])
                send(from_b.at[turn, rows, :], pair_b.at[turn, rows, :], pass_send.at[1, turn], pass_recv.at[1, turn], partner).start()
        return carry
    lax.fori_loop(0, 5, hand_on, 0)

    def dirs_done(turn, carry):
        for part in (0, 1):
            ref = own.at[turn, pl.ds(0, ROWS_OF[part]), :]

            @pl.when(tall_of(my_chip, core, turn) == part)
            def _():
                for lane in range(4):
                    wait_bytes(ref, dir_send.at[lane, turn])
            for sem, chip, its_core in ((dir_recv.at[0, turn], my_chip, 1 - core), (pass_send.at[0, turn], a_chip, core),
                                        (pass_send.at[1, turn], b_chip, core), (pass_recv.at[0, turn], b_chip, 1 - core),
                                        (pass_recv.at[1, turn], a_chip, 1 - core)):
                @pl.when(tall_of(chip, its_core, turn) == part)
                def _():
                    wait_bytes(ref, sem)
        return carry
    lax.fori_loop(0, 5, dirs_done, 0)


def step_blocks(n_dev, x_in, dy_mid, x_mid, dy_out, root_left, root_right, graft_sq, momentum, stat_left, stat_right):
    tokens, n_model = x_in.shape
    piece = jax.ShapeDtypeStruct((5, 2, BLK, HALF), F32)
    tile = jax.ShapeDtypeStruct((5, BLK, BLK), F32)
    dirs, early, late = (jax.ShapeDtypeStruct((k, BLK, BLK), BF16) for k in (5, EARLY, 5 - EARLY))
    dma = pltpu.SemaphoreType.DMA
    outs = pl.pallas_call(
        functools.partial(step_kernel, 1.0 / n_dev),
        out_shape=(piece, piece, piece, tile, tile, tile, tile, dirs, dirs, early, late, dirs, dirs, dirs),
        in_specs=[ANY] * 10,
        out_specs=(ANY,) * 14,
        scratch_shapes=[
            pltpu.VMEM((2, tokens, n_model), BF16),
            pltpu.VMEM((3, tokens, HALF), BF16),
            pltpu.VMEM((2, n_model, HALF), F32),
            pltpu.VMEM((STRIPS, n_model, HALF), F32),
            pltpu.VMEM((12, BLK, HALF), F32),
            pltpu.VMEM((3, 2, BLK, HALF), F32),
            pltpu.VMEM((6, BLK, BLK), F32),
            pltpu.VMEM((BLK, BLK), F32),
            pltpu.VMEM((BLK, BLK), F32),
            dma((2,)), dma((3,)), dma((2,)), dma((STRIPS,)), dma((2 * STRIPS,)), dma((12,)), dma((5, 2)), dma((5, 2)), dma((5,)),
            dma((3,)), dma((6,)), dma((4,)), dma((4, 5)), dma((3, 5)), dma((2, 5)), dma((2, 5)),
        ],
        compiler_params=pltpu.CompilerParams(collective_id=0, has_side_effects=True, vmem_limit_bytes=VMEM_MAX),
        name='step_blocks',
    )(x_in, dy_mid, x_mid, dy_out, root_left, root_right, graft_sq, momentum, stat_left, stat_right)
    return outs[3:]


def pass_kernel(*refs):
    for src, dst in zip(refs[:4], refs[4:]):
        dst[...] = src[...]


def pass_on(states):
    spec = pl.BlockSpec((1, BLK, BLK), lambda i: (i, 0, 0))
    return pl.pallas_call(
        pass_kernel,
        grid=(states[0].shape[0],),
        out_shape=tuple(jax.ShapeDtypeStruct(x.shape, x.dtype) for x in states),
        in_specs=[spec] * 4,
        out_specs=(spec,) * 4,
        compiler_params=pltpu.CompilerParams(vmem_limit_bytes=VMEM_MAX),
        cost_estimate=pl.CostEstimate(flops=10 ** 10, bytes_accessed=42 * 10 ** 6, transcendentals=0),
        name='pass_on',
    )(*states)


BUFS, AHEAD = 4, 3


def apply_kernel(places, *refs):
    n_src = len(places)
    srcs, (w1, w2) = refs[:n_src], refs[n_src:n_src + 2]
    outs = refs[-8:-6]
    dir_buf, w_buf, o_buf, dir_sem, w_sem, o_sem = refs[-6:]
    me = lax.axis_index('dp')
    core, my_chip = me % 2, me // 2
    x_chip, y_chip, far_chip = flip(me, 2) // 2, flip(me, 4) // 2, flip(me, 6) // 2
    a_chip, b_chip = jnp.where(core == 0, x_chip, y_chip), jnp.where(core == 0, y_chip, x_chip)
    chips = dict(own=my_chip, a=a_chip, b=b_chip, far=far_chip)
    counts = [src.shape[0] for src in srcs]
    starts = [sum(counts[:k]) for k in range(n_src)]
    n_tiles = sum(counts)

    def tile(n):
        which, spot, turn, chip, its_core = 0, n, n + places[0][2], chips[places[0][0]], core if places[0][1] else 1 - core
        for k, (name, same, begin) in enumerate(places):
            here = n >= starts[k]
            which = jnp.where(here, k, which)
            spot = jnp.where(here, n - starts[k], spot)
            turn = jnp.where(here, n - starts[k] + begin, turn)
            chip = jnp.where(here, chips[name], chip)
            its_core = jnp.where(here, core if same else 1 - core, its_core)
        strip, tall = tile_at(chip, 5 * its_core + slot_at(chip, its_core, turn))
        return which, spot, chip, strip, tall

    def window(n, do):
        _, _, chip, strip, tall = tile(n)
        for tall_k in (0, 1):
            for last in (0, 1):
                big, small = ROWS_OF[tall_k], (512, 256)[last]
                at = pl.multiple_of(strip * BLK, BLK)
                here = (tall == tall_k) & ((strip == 9) == (last == 1))

                @pl.when(here & (chip < 2))
                def _():
                    do(0, (pl.ds(tall_k * BLK, big), pl.ds(at, small)), (pl.ds(0, big), pl.ds(0, small)))

                @pl.when(here & (chip >= 2))
                def _():
                    do(1, (pl.ds(at, small), pl.ds(tall_k * BLK, big)), (pl.ds(0, small), pl.ds(0, big)))

    def load(n):
        which, turn, _, _, _ = tile(n)
        slot = n % BUFS
        for k, src in enumerate(srcs):
            @pl.when(which == k)
            def _():
                pltpu.make_async_copy(src.at[turn], dir_buf.at[slot], dir_sem.at[slot]).start()
        window(n, lambda k, at, view: pltpu.make_async_copy((w1, w2)[k].at[at], w_buf.at[slot].at[view], w_sem.at[slot]).start())

    def load_wait(n):
        slot = n % BUFS
        wait_bytes(dir_buf.at[slot], dir_sem.at[slot])
        window(n, lambda k, at, view: wait_bytes(w_buf.at[slot].at[view], w_sem.at[slot]))

    def store_wait(n):
        slot = n % BUFS
        window(n, lambda k, at, view: wait_bytes(o_buf.at[slot].at[view], o_sem.at[slot]))

    for n in range(AHEAD):
        load(n)

    def step(n, carry):
        slot = n % BUFS

        @pl.when(n + AHEAD < n_tiles)
        def _():
            load(n + AHEAD)
        load_wait(n)

        @pl.when(n >= BUFS)
        def _():
            store_wait(n - BUFS)
        chip = tile(n)[2]

        @pl.when(chip < 2)
        def _():
            o_buf[slot] = w_buf[slot] - LEARN_RATE * (dir_buf[slot].astype(F32) + WEIGHT_DECAY * w_buf[slot])

        @pl.when(chip >= 2)
        def _():
            o_buf[slot] = w_buf[slot] - LEARN_RATE * (dir_buf[slot].astype(F32).T + WEIGHT_DECAY * w_buf[slot])
        window(n, lambda k, at, view: pltpu.make_async_copy(o_buf.at[slot].at[view], outs[k].at[at], o_sem.at[slot]).start())
        return carry
    lax.fori_loop(0, n_tiles, step, 0)
    for n in range(n_tiles - BUFS, n_tiles):
        store_wait(n)


def apply_update(places, srcs, w1, w2, partial=()):
    dma = pltpu.SemaphoreType.DMA
    n_in = len(srcs) + 2
    share = sum(src.shape[0] for src in srcs) / 40
    return pl.pallas_call(
        functools.partial(apply_kernel, places),
        out_shape=(jax.ShapeDtypeStruct(w1.shape, F32), jax.ShapeDtypeStruct(w2.shape, F32)),
        in_specs=[ANY] * (n_in + len(partial)),
        out_specs=(ANY, ANY),
        scratch_shapes=[
            pltpu.VMEM((BUFS, BLK, BLK), BF16), pltpu.VMEM((BUFS, BLK, BLK), F32), pltpu.VMEM((BUFS, BLK, BLK), F32),
            dma((BUFS,)), dma((BUFS,)), dma((BUFS,)),
        ],
        input_output_aliases={n_in: 0, n_in + 1: 1} if partial else {},
        compiler_params=pltpu.CompilerParams(vmem_limit_bytes=VMEM_MAX),
        cost_estimate=pl.CostEstimate(flops=int(share * 20 * 10 ** 9), bytes_accessed=int(share * 88 * 10 ** 6), transcendentals=0),
        name='apply_update',
    )(*srcs, w1, w2, *partial)


def solution(mesh):
    n_dev = mesh.shape['dp']
    swap = [(i, i ^ 1) for i in range(n_dev)]
    onward = [(i, i ^ (4 if i % 2 == 0 else 2)) for i in range(n_dev)]

    def per_device(x_in, dy_mid, x_mid, dy_out, w_fc1, w_fc2, stat_left, stat_right, root_left, root_right, graft_sq, momentum):
        *states, own, pair, from_a, from_c, from_b, pair_a, pair_b = step_blocks(
            n_dev, x_in, dy_mid, x_mid, dy_out, root_left, root_right, graft_sq, momentum, stat_left, stat_right)
        far = lax.ppermute(from_a, 'dp', onward)
        far_late = lax.ppermute(from_c, 'dp', onward)
        near = (('own', True, 0), ('own', False, 0), ('a', True, 0), ('a', True, EARLY), ('b', True, 0), ('b', False, 0), ('a', False, 0))
        partial = apply_update(near, (own, pair, from_a, from_c, from_b, pair_a, pair_b), w_fc1, w_fc2)
        far, partial, *states = lax.optimization_barrier((far, partial, *states))
        pair_far = lax.ppermute(far, 'dp', swap)
        new_left, new_right, new_sq, new_mom = pass_on(states)
        partial = apply_update((('far', True, 0), ('far', False, 0)), (far, pair_far), w_fc1, w_fc2, partial)
        pair_far_late = lax.ppermute(far_late, 'dp', swap)
        new_w1, new_w2 = apply_update((('far', True, EARLY), ('far', False, EARLY)), (far_late, pair_far_late), w_fc1, w_fc2, partial)
        return new_w1, new_w2, new_left, new_right, new_sq, new_mom

    row_spec = P('dp', None)
    rep_spec = P(None, None)
    tile_spec = P('dp', None, None)
    in_specs = (row_spec, row_spec, row_spec, row_spec, rep_spec, rep_spec, tile_spec, tile_spec, tile_spec, tile_spec, tile_spec, tile_spec)
    out_specs = (rep_spec, rep_spec, tile_spec, tile_spec, tile_spec, tile_spec)
    return jax.shard_map(per_device, mesh=mesh, in_specs=in_specs, out_specs=out_specs, check_vma=False)
```

time: 909 us -> 276 us (0.30); the launches traced: 895 us -> 276 us
  local copies, waits for them, and re-layouts: 357 us -> 0 us
  waiting for transfers between devices: 290 us -> 5.61 us
  Pallas kernels: 0 us -> 265 us
  matrix products: 166 us -> 0 us
  other arithmetic: 67.3 us -> 0 us
  between operations: 14.6 us -> 0.85 us
    pallas_call x0 -> x5, Pallas kernels: none -> 265 us  [the longest x1 216 us: step_blocks(): pl.pallas_call(functools.partial(step_kernel, 1.0 / n_dev), out_shape=(pi...]
    unnamed x3 -> x0, waiting for transfers between devices: 238 us -> none
    unnamed x20 -> x0, local copies, waits for them, and re-layouts: 180 us -> none
    dot_general x6 -> x0, matrix products: 166 us -> none  [the longest x2 104 us: grad_blocks(): jnp.einsum('tri,tcj->rcij', x_pad, dy_pad, preferred_element_type=jnp.flo...]
    pad x4 -> x0, local copies, waits for them, and re-layouts: 70.8 us -> none  [the longest x2 35.4 us: grad_blocks(): jnp.pad(x_rows, ((0, 0), (0, in_blocks * block_dim - n_in)))]
    transpose x3 -> x0, local copies, waits for them, and re-layouts: 64.7 us -> none  [the longest x2 44.3 us: grad_blocks(): jnp.einsum('tri,tcj->rcij', x_pad, dy_pad, preferred_element_type=jnp.flo...]
    all_gather x1 -> x0, waiting for transfers between devices: 51.9 us -> none  [per_device(): lax.all_gather(new_mom.astype(jnp.bfloat16), 'dp', axis=0, tiled=True)]
    sub x2 -> x0, other arithmetic: 28.9 us -> none  [the longest x1 14.4 us: apply_update(): w_fc1 - LEARN_RATE * (dir_fc1.astype(jnp.float32) + WEIGHT_DECAY * w_fc1)]
  transfers between devices with their start and end apart: 2 -> 4, of which waited for: 2 -> 1; matrix products, arithmetic and copies ran while one was open for 6% -> 0% of each run, Pallas kernels for 0% -> 17%
where the time goes in v2:
time: 276 us
  Pallas kernels  265 us (96%)
  waiting for transfers between devices  5.61 us (2%)
  starting transfers between devices  4.12 us (1%)
    pallas_call x1, Pallas kernels, step_blocks(): pl.pallas_call(functools.partial(step_kernel, 1.0 / n_dev), out_shape=(pi...  216 us
    pallas_call x3, Pallas kernels, apply_update(): pl.pallas_call(functools.partial(apply_kernel, places), out_shape=(jax.Sh...  34 us
    pallas_call x1, Pallas kernels, pass_on(): pl.pallas_call(pass_kernel, grid=(states[0].shape[0],), out_shape=tuple((...  15.6 us
    ppermute x1, waiting for transfers between devices, per_device(): far_late = lax.ppermute(from_c, 'dp', onward)  5.6 us
  transfers between devices with their start and end apart: 4, of which 1 were waited for; matrix products, arithmetic and copies ran while one was open for 0% of the time, Pallas kernels for 17%

profile of v2, /device:TPU:0, one launch (start us, length us, event | category | flops | bytes accessed | tf_op | source)
XLA Modules:
  0.0 275.9 jit_solution(6174927419944510)
XLA Ops:
  0.6 215.7 %step_blocks.1 = (f32[5,2,512,256]{3,2,1,0:T(8,128)}, f32[5,2,512,256]{3,2,1,0:T(8,128)}, f32[5,2,512,256]{3,2,1,0:T(8,128)}, f32[5,512,512]{2,1,0:T(8,128)}, f3...) custom-call(bf16[4096,896]{1,0:T(8,128)(2,1)} %x_in.1, ...), custom_call_target="tpu_custom_call" | custom-call | tf_op jit(solution)/shard_map/step_blocks/pallas_call | solution.py:452
  216.4 4.1 %collective-permute-start.2 = (bf16[3,512,512]{2,1,0:T(8,128)(2,1)}, bf16[3,512,512]{2,1,0:T(8,128)(2,1)}, u32[]{:S(2)}, u32[]{:S(2)}) collective-permute-start(bf16[3,512,512]{2,1,0:T(8,128)(2,1)} %get-tuple-element.35.refs_2_), channel_id=1, source_target_pairs={{0,4},{1,3},{2,6},{3,1},{4,0},{5,7},{6,2},{7,5}} | collective-permute-start | bytes 4718600 | tf_op jit(solution)/shard_map/ppermute | solution.py:616
  220.4 0.0 collective-permute-start
  220.5 23.9 %apply_update.3 = (f32[896,4864]{1,0:T(8,128)}, f32[4864,896]{1,0:T(8,128)}) custom-call(bf16[5,512,512]{2,1,0:T(8,128)(2,1)} %get-tuple-element.36.refs_0_, bf16[5,512,512]{2,1,0:T(8,128)(2,1)} %get-tuple-element.37.refs_1_, bf16[3,512,512]{2,1,0:T(8,128)(2,1)} %get-tuple-element.35.refs_2_, bf16[2,512,512]{2,1,0:T(8,128)(2,1)} %get-tuple-element.34.refs_3_, ...), custom_call_target="tpu_custom_call" | custom-call | flops 15000000512 | bytes 66000000 | tf_op jit(solution)/shard_map/apply_update/pallas_call | solution.py:592
  244.4 0.0 collective-permute-done.2.refs_0_
  244.4 0.0 collective-permute-start.3
  244.5 5.6 %collective-permute-done.refs_0_ = bf16[2,512,512]{2,1,0:T(8,128)(2,1)} collective-permute-done((bf16[2,512,512]{2,1,0:T(8,128)(2,1)}, bf16[2,512,512]{2,1,0:T(8,128)(2,1)}, u32[]{:S(2)}, u32[]{:S(2)}) %collective-permute-start) | collective-permute-done | bytes 1048608 | tf_op jit(solution)/shard_map/ppermute | solution.py:617
  250.1 0.0 collective-permute-start.1
  250.1 15.6 %pass_on.1 = (f32[5,512,512]{2,1,0:T(8,128)}, f32[5,512,512]{2,1,0:T(8,128)}, f32[5,512,512]{2,1,0:T(8,128)}, f32[5,512,512]{2,1,0:T(8,128)}) custom-call(f32[5,512,512]{2,1,0:T(8,128)} %get-tuple-element.54.refs_0_, f32[5,512,512]{2,1,0:T(8,128)} %get-tuple-element.55.refs_1_, f32[5,512,512]{2,1,0:T(8,128)} %get-tuple-element.56.refs_2_, ...), custom_call_target="tpu_custom_call" | custom-call | flops 10000000000 | bytes 42000000 | tf_op jit(solution)/shard_map/pass_on/pallas_call | solution.py:483
  265.6 0.0 collective-permute-done.3.refs_1_
  265.6 6.2 %apply_update.4 = (f32[896,4864]{1,0:T(8,128)}, f32[4864,896]{1,0:T(8,128)}) custom-call(bf16[3,512,512]{2,1,0:T(8,128)(2,1)} %collective-permute-done.2.refs_0_, bf16[3,512,512]{2,1,0:T(8,128)(2,1)} %collective-permute-done.3.refs_1_, f32[896,4864]{1,0:T(8,128)} %refs_2_.3, f32[4864,896]{1,0:T(8,128)} %refs_3_.3, ...), custom_call_target="tpu_custom_call", output_to_operand_aliasing={{0}: (4, {}), {1}: (5, {})} | custom-call | flops 3000000000 | bytes 13200000 | tf_op jit(solution)/shard_map/apply_update/pallas_call | solution.py:592
  271.8 0.0 collective-permute-done.1.refs_1_
  271.8 3.9 %apply_update.5 = (f32[896,4864]{1,0:T(8,128)}, f32[4864,896]{1,0:T(8,128)}) custom-call(bf16[2,512,512]{2,1,0:T(8,128)(2,1)} %collective-permute-done.refs_0_, bf16[2,512,512]{2,1,0:T(8,128)(2,1)} %collective-permute-done.1.refs_1_, f32[896,4864]{1,0:T(8,128)} %refs_2_.3, f32[4864,896]{1,0:T(8,128)} %refs_3_.3, ...), custom_call_target="tpu_custom_call", output_to_operand_aliasing={{0}: (4, {}), {1}: (5, {})} | custom-call | flops 2000000000 | bytes 8800000 | tf_op jit(solution)/shard_map/apply_update/pallas_call | solution.py:592
Async XLA Ops:
  216.4 28.0 %collective-permute-start.2 = (bf16[3,512,512]{2,1,0:T(8,128)(2,1)}, bf16[3,512,512]{2,1,0:T(8,128)(2,1)}, u32[]{:S(2)}, u32[]{:S(2)}) collective-permute-start(bf16[3,512,512]{2,1,0:T(8,128)(2,1)} %get-tuple-element.35.refs_2_), channel_id=1, source_target_pairs={{0,4},{1,3},{2,6},{3,1},{4,0},{5,7},{6,2},{7,5}} | collective-permute-start | bytes 4718600 | tf_op jit(solution)/shard_map/ppermute | solution.py:616
  220.4 29.6 %collective-permute-start = (bf16[2,512,512]{2,1,0:T(8,128)(2,1)}, bf16[2,512,512]{2,1,0:T(8,128)(2,1)}, u32[]{:S(2)}, u32[]{:S(2)}) collective-permute-start(bf16[2,512,512]{2,1,0:T(8,128)(2,1)} %get-tuple-element.34.refs_3_), channel_id=1, source_target_pairs={{0,4},{1,3},{2,6},{3,1},{4,0},{5,7},{6,2},{7,5}} | collective-permute-start | bytes 3145736 | tf_op jit(solution)/shard_map/ppermute | solution.py:617
  244.4 21.2 %collective-permute-start.3 = (bf16[3,512,512]{2,1,0:T(8,128)(2,1)}, bf16[3,512,512]{2,1,0:T(8,128)(2,1)}, u32[]{:S(2)}, u32[]{:S(2)}) collective-permute-start(bf16[3,512,512]{2,1,0:T(8,128)(2,1)} %collective-permute-done.2.refs_0_), channel_id=1, source_target_pairs={{0,1},{1,0},{2,3},{3,2},{4,5},{5,4},{6,7},{7,6}} | collective-permute-start | bytes 4718600 | tf_op jit(solution)/shard_map/ppermute | solution.py:621
  250.1 21.7 %collective-permute-start.1 = (bf16[2,512,512]{2,1,0:T(8,128)(2,1)}, bf16[2,512,512]{2,1,0:T(8,128)(2,1)}, u32[]{:S(2)}, u32[]{:S(2)}) collective-permute-start(bf16[2,512,512]{2,1,0:T(8,128)(2,1)} %collective-permute-done.refs_0_), channel_id=1, source_target_pairs={{0,1},{1,0},{2,3},{3,2},{4,5},{5,4},{6,7},{7,6}} | collective-permute-start | bytes 3145736 | tf_op jit(solution)/shard_map/ppermute | solution.py:624
